TPU v7x, 128 devices: a whole 4x4x4 slice. The times are simulated.
128 devices in a mesh: grp: 8 (over x, z_lo), mem: 16 (over z_hi, y, core).
Axes of the slice: x: 4, y: 4, z: 4 (z_hi: 2, z_lo: 2; z = z_hi * 2 + z_lo), core: 2. Of those that a mesh axis runs over, the one named last changes fastest.
Arguments:
- weight: bfloat16 [4, 8192, 16384], P(None, None, ('grp', 'mem')), may hold values from -0.046875 to 0.046875
- activation: bfloat16 [2, 16384, 512], P(None, ('grp', 'mem')), may hold values from -6 to 6
- points: int32 [8], replicated, may hold values from 0 to 7, each once
Outputs:
- share: float32 [8, 8192, 512], P('grp', 'mem')
Inputs may be any that keep to these rules, and one draw needn't show every extreme that they name: A permutation of 0 to 7; group g evaluates at points[g] + 1.
All inputs are finite; a program needn't handle non-finite values.
Results may differ from a plain program's by a relative error of at most 0.0042.
Values may be sent and summed in bfloat16 or wider, within the bound.
A program may use at most 320 MiB of HBM per device.

v0:
```python
import jax
import jax.numpy as jnp
from jax import lax
from jax.sharding import PartitionSpec as P


def cut_along(shard, dim, count):
    lengths = shard.shape
    pieces = shard.reshape(*lengths[:dim], count, lengths[dim] // count, *lengths[dim + 1 :])
    return jnp.moveaxis(pieces, dim, 0)


def sum_at_owner(shard, axis, dim):
    pieces = cut_along(shard, dim, lax.axis_size(axis))
    arrived = lax.all_to_all(pieces, axis, split_axis=0, concat_axis=0, tiled=True)
    return arrived.astype(jnp.float32).sum(axis=0)


def code_stack(raw_blocks, factors):
    total = factors[:, 0, None, None] * raw_blocks[0].astype(jnp.float32)[None]
    for block in range(1, raw_blocks.shape[0]):
        total = total + factors[:, block, None, None] * raw_blocks[block].astype(jnp.float32)[None]
    return total.astype(jnp.bfloat16)


def per_device(weight, activation, points):
    groups = lax.axis_size("grp")
    blocks = weight.shape[0]
    splits = activation.shape[0]
    anchors = (points + 1).astype(jnp.float32) / groups
    factors = anchors[:, None] ** jnp.arange(blocks, dtype=jnp.float32)[None, :]
    lifts_all = anchors[:, None] ** (jnp.arange(splits, dtype=jnp.float32) * blocks)[None, :]
    slab = lax.all_to_all(weight, "mem", split_axis=1, concat_axis=2, tiled=True)
    block_input = lax.all_gather(activation, "mem", axis=1, tiled=True)
    coded_weight = code_stack(slab, factors)
    coded_input = code_stack(block_input, lifts_all)
    return sum_at_owner(
        jnp.einsum(
            "grk,gkc->grc", coded_weight, coded_input, preferred_element_type=jnp.float32
        ).astype(jnp.bfloat16),
        "grp",
        0,
    )


def solution(mesh):
    placed = (P(None, None, ("grp", "mem")), P(None, ("grp", "mem"), None), P())
    return jax.shard_map(
        per_device, mesh=mesh, in_specs=placed, out_specs=P("grp", "mem", None), check_vma=False
    )
```

profile of v0, /device:TPU:1, one launch (start us, length us, event | category | flops | bytes accessed | tf_op | source)
XLA Modules:
  0.0 304.5 jit_solution(15348108280595390962)
XLA Ops:
  6.5 12.2 %copy.16 = bf16[4,8192,128]{2,0,1:T(4,128)(2,1)} copy(bf16[4,8192,128]{2,1,0:T(8,128)(2,1)} %param.3) | data formatting | bytes 16777216 | tf_op args[0]
  18.7 0.0 copy-start.3
  18.7 9.4 %all-to-all-start = ((bf16[4,8192,128]{2,0,1:T(4,128)(2,1)}), bf16[4,8192,128]{2,0,1:T(4,128)(2,1)}, u32[]{:S(2)}, u32[]{:S(2)}) async-start(bf16[4,8192,128]{2,0,1:T(4,128)(2,1)} %copy.16), calls=%async_computation | async-start | bytes 16777216 | tf_op jit(solution)/shard_map/all_to_all | solution.py:33
  28.1 0.0 all-gather.2.cloned.1.call-start
  28.2 0.7 all-gather.2.cloned.1.call-update
  28.9 0.0 copy-done.3
  28.9 0.1 broadcast_power_fusion
  29.0 117.9 %all-to-all-done = bf16[4,8192,128]{2,0,1:T(4,128)(2,1)} async-done(((bf16[4,8192,128]{2,0,1:T(4,128)(2,1)}), bf16[4,8192,128]{2,0,1:T(4,128)(2,1)}, u32[]{:S(2)}, u32[]{:S(2)}) %all-to-all-start) | async-done | bytes 8388640 | tf_op jit(solution)/shard_map/all_to_all | solution.py:33
  146.9 7.8 %copy.17 = bf16[4,8192,128]{2,1,0:T(8,128)(2,1)} copy(bf16[4,8192,128]{2,0,1:T(4,128)(2,1)} %all-to-all-done) | data formatting | bytes 16777216 | tf_op jit(solution)/shard_map/all_to_all | solution.py:33
  154.7 10.0 %slice_convert_fusion.3 = (f32[1,512,16,128]{3,1,2,0:T(8,128)}, f32[1,512,16,128]{3,1,2,0:T(8,128)}, f32[1,512,16,128]{3,1,2,0:T(8,128)}, f32[1,512,16,128]{3,1,2,0:T(8,128)}) fusion(bf16[4,512,16,128]{3,1,2,0:T(8,128)(2,1)} %bitcast.34), kind=kLoop, calls=%fused_computation.24 | loop fusion | flops 4194304 | bytes 25165824 | tf_op jit(solution)/shard_map/convert_element_type | solution.py:20
  164.6 5.4 %copy.18 = f32[1,512,16,128]{1,3,2,0:T(8,128)} copy(f32[1,512,16,128]{3,1,2,0:T(8,128)} %get-tuple-element.5) | data formatting | bytes 8388608 | tf_op jit(solution)/shard_map/convert_element_type | solution.py:20
  170.0 5.5 %copy.19 = f32[512,2048]{1,0:T(8,128)} copy(f32[512,2048]{0,1:T(8,128)} %bitcast.35) | data formatting | bytes 8388608 | tf_op jit(solution)/shard_map/convert_element_type | solution.py:20
  175.5 5.4 %copy.20 = f32[1,512,16,128]{1,3,2,0:T(8,128)} copy(f32[1,512,16,128]{3,1,2,0:T(8,128)} %get-tuple-element.8) | data formatting | bytes 8388608 | tf_op jit(solution)/shard_map/convert_element_type | solution.py:22
  180.8 5.4 %copy.21 = f32[512,2048]{1,0:T(8,128)} copy(f32[512,2048]{0,1:T(8,128)} %bitcast.36) | data formatting | bytes 8388608 | tf_op jit(solution)/shard_map/convert_element_type | solution.py:22
  186.3 5.4 %copy.22 = f32[1,512,16,128]{1,3,2,0:T(8,128)} copy(f32[1,512,16,128]{3,1,2,0:T(8,128)} %get-tuple-element.7) | data formatting | bytes 8388608 | tf_op jit(solution)/shard_map/convert_element_type | solution.py:22
  191.6 5.4 %copy.23 = f32[512,2048]{1,0:T(8,128)} copy(f32[512,2048]{0,1:T(8,128)} %bitcast.37) | data formatting | bytes 8388608 | tf_op jit(solution)/shard_map/convert_element_type | solution.py:22
  197.0 5.4 %copy.24 = f32[1,512,16,128]{1,3,2,0:T(8,128)} copy(f32[1,512,16,128]{3,1,2,0:T(8,128)} %get-tuple-element.6) | data formatting | bytes 8388608 | tf_op jit(solution)/shard_map/convert_element_type | solution.py:22
  202.4 5.4 %copy.25 = f32[512,2048]{1,0:T(8,128)} copy(f32[512,2048]{0,1:T(8,128)} %bitcast.38) | data formatting | bytes 8388608 | tf_op jit(solution)/shard_map/convert_element_type | solution.py:22
  207.8 0.0 all-gather.2.cloned.1.call-done
  207.8 0.0 copy-start
  207.8 0.0 copy-start.1
  207.9 0.0 copy-start.2
  207.9 7.7 %fusion.14 = (f32[2048,512]{1,0:T(8,128)}, f32[2048,512]{1,0:T(8,128)}) fusion(bf16[2,2048,512]{2,1,0:T(8,128)(2,1)} %all-gather.2.cloned.1.call-done), kind=kLoop, calls=%fused_computation.20 | loop fusion | flops 2097152 | bytes 12582912 | tf_op jit(solution)/shard_map/mul | solution.py:20
  215.6 0.0 copy-done
  215.6 0.0 copy-done.1
  215.6 1.1 copy-done.2
  216.7 26.3 %convert_bitcast_fusion = bf16[8,1,512,512]{3,2,1,0:T(8,128)(2,1)} fusion(f32[2048,512]{1,0:T(8,128)} %get-tuple-element.10, f32[8]{0:T(128)S(1)} %get-tuple-element.16, f32[2048,512]{1,0:T(8,128)} %get-tuple-element.9, f32[8]{0:T(128)S(1)} %get-tuple-element.15, f32[512,2048]{1,0:T(8,128)} %copy.25, f32[8]{0:T(128)S(1)} %get-tuple-element.19, ...), kind=kOutput, calls=%fused_computation.16 | convolution fusion | flops 8692695040 | bytes 29360320 | tf_op jit(solution)/shard_map/grk,gkc->grc/dot_general | solution.py:38
  243.0 53.1 %all_to_all.20 = bf16[8,1,512,512]{3,2,1,0:T(8,128)(2,1)S(1)} all-to-all(bf16[8,1,512,512]{3,2,1,0:T(8,128)(2,1)} %convert_bitcast_fusion), channel_id=1, replica_groups=mesh['grp'=8,'mem'=16] {'grp'}, dimensions={0} | all-to-all | bytes 8388608 | tf_op jit(solution)/shard_map/all_to_all | solution.py:15
  296.1 1.6 convert_reduce_fusion
  (4 shorter events, 0.0 us)
Async XLA Ops:
  18.7 10.2 %copy-start.3 = (s32[8]{0:T(128)S(1)}, s32[8]{0:T(128)}, u32[]{:S(2)}) copy-start(s32[8]{0:T(128)} %param.5) | copy-start | bytes 100
  18.7 128.2 %all-to-all-start = ((bf16[4,8192,128]{2,0,1:T(4,128)(2,1)}), bf16[4,8192,128]{2,0,1:T(4,128)(2,1)}, u32[]{:S(2)}, u32[]{:S(2)}) async-start(bf16[4,8192,128]{2,0,1:T(4,128)(2,1)} %copy.16), calls=%async_computation | async-start | bytes 16777216 | tf_op jit(solution)/shard_map/all_to_all | solution.py:33
  28.1 179.7 %all-gather.2.cloned.1.call-start = ((), (), s32[]{:S(2)}) async-start(), calls=%async_computation.2 | async-start | bytes 4456448 | tf_op jit(solution)/shard_map/all_gather | solution.py:34
  207.8 7.7 %copy-start = (f32[512,2048]{1,0:T(8,128)S(1)}, f32[512,2048]{1,0:T(8,128)}, u32[]{:S(2)}) copy-start(f32[512,2048]{1,0:T(8,128)} %copy.19) | copy-start | bytes 12582916
  207.8 7.7 %copy-start.1 = (f32[512,2048]{1,0:T(8,128)S(1)}, f32[512,2048]{1,0:T(8,128)}, u32[]{:S(2)}) copy-start(f32[512,2048]{1,0:T(8,128)} %copy.21) | copy-start | bytes 12582916
  207.9 8.8 %copy-start.2 = (f32[512,2048]{1,0:T(8,128)S(1)}, f32[512,2048]{1,0:T(8,128)}, u32[]{:S(2)}) copy-start(f32[512,2048]{1,0:T(8,128)} %copy.23) | copy-start | bytes 12582916
Sparse Core Ops, SparseCore 0:
  31.4 123.3 all-gather.1
where the time goes:
time: 306 us; the launch traced here: 305 us
  waiting for transfers between devices  119 us (39%)
  local copies, waits for them, and re-layouts  64.4 us (21%)
  blocking collectives  53.1 us (17%)
  matrix products  26.3 us (9%)
  other arithmetic  19.2 us (6%)
  between operations  13.5 us (4%)
  starting transfers between devices  9.46 us (3%)
    all_to_all x1, waiting for transfers between devices, per_device(): lax.all_to_all(weight, 'mem', split_axis=1, concat_axis=2, tiled=True)  118 us
    all_to_all x1, blocking collectives, sum_at_owner(): lax.all_to_all(pieces, axis, split_axis=0, concat_axis=0, tiled=True)  53.1 us
    convert_element_type x6, local copies, waits for them, and re-layouts, code_stack(): raw_blocks[block].astype(jnp.float32)[None]  32.4 us
    dot_general x1, matrix products, per_device(): jnp.einsum('grk,gkc->grc', coded_weight, coded_input, preferred_element_t...  26.3 us
    unnamed x9, local copies, waits for them, and re-layouts  13.3 us
    convert_element_type x2, local copies, waits for them, and re-layouts, code_stack(): total = factors[:, 0, None, None] * raw_blocks[0].astype(jnp.float32)[None]  10.8 us
    convert_element_type x1, other arithmetic, code_stack(): total = factors[:, 0, None, None] * raw_blocks[0].astype(jnp.float32)[None]  9.95 us
    all_to_all x1, starting transfers between devices, per_device(): lax.all_to_all(weight, 'mem', split_axis=1, concat_axis=2, tiled=True)  9.42 us
  transfers between devices with their start and end apart: 2, of which 1 were waited for; matrix products, arithmetic and copies ran while one was open for 20% of the time, Pallas kernels for 0%

commit v1 on v0

v1 whole, which is shorter than its diff:
```python
import functools

import jax
import jax.numpy as jnp
from jax import lax
from jax.experimental import pallas as pl
from jax.experimental.pallas import tpu as pltpu
from jax.sharding import PartitionSpec as P

MESH = pl.DeviceIdType.MESH
ROWS = 512
WIDTH = 32
STEPS = ROWS // WIDTH
AHEAD = 3
LAG = 2


def place():
    grp, mem = lax.axis_index("grp"), lax.axis_index("mem")
    return grp // 2, (mem // 2) % 4, (mem // 8) * 2 + grp % 2, mem % 2


def device(x, y, z, core):
    return (x * 2 + z % 2, (z // 2) * 8 + y * 2 + core)


def kernel(weight, act, points, out, slab, feats, prods, sent, got, total,
           slab_sem, slab_out, feat_sem, feat_out, got_sem, got_out, own_sem, out_sem):
    x, y, z, core = place()
    line = [(dy, dc) for dy in (2, 1, 3, 0) for dc in (0, 1) if dy or dc]
    plane = [(dx, dz) for dx in (2, 1, 3, 0) for dz in (2, 1, 3, 0) if dx or dz]
    mine = y * 2 + core
    spot = x * 4 + z

    def line_peer(dy, dc):
        return lax.rem(y + dy, 4), lax.rem(core + dc, 2)

    def plane_peer(dx, dz):
        return lax.rem(x + dx, 4), lax.rem(z + dz, 4)

    barrier = pltpu.get_barrier_semaphore()
    for dy, dc in line:
        py, pc = line_peer(dy, dc)
        pl.semaphore_signal(barrier, inc=1, device_id=device(x, py, z, pc), device_id_type=MESH)
    for dx, dz in plane:
        px, pz = plane_peer(dx, dz)
        pl.semaphore_signal(barrier, inc=1, device_id=device(px, y, pz, core), device_id_type=MESH)
    pl.semaphore_wait(barrier, len(line) + len(plane))

    def lanes(index):
        return pl.ds(pl.multiple_of(index * 128, 128), 128)

    def feat_slot(index):
        return feats.at[:, lanes(index), :]

    def feat_copy(source, index, py, pc, order):
        return pltpu.make_async_remote_copy(
            src_ref=source, dst_ref=feat_slot(index), send_sem=feat_out.at[order],
            recv_sem=feat_sem.at[index], device_id=device(x, py, z, pc), device_id_type=MESH)

    def slab_copy(step, dy, dc):
        py, pc = line_peer(dy, dc)
        start = pl.multiple_of((py * 2 + pc) * ROWS + step * WIDTH, WIDTH)
        return pltpu.make_async_remote_copy(
            src_ref=weight.at[:, :, pl.ds(start, WIDTH), :],
            dst_ref=slab.at[step, :, :, :, lanes(mine)],
            send_sem=slab_out.at[step, dy * 2 + dc], recv_sem=slab_sem.at[step, mine],
            device_id=device(x, py, z, pc), device_id_type=MESH)

    def slab_own(step):
        start = pl.multiple_of(mine * ROWS + step * WIDTH, WIDTH)
        return pltpu.make_async_copy(
            weight.at[:, :, pl.ds(start, WIDTH), :], slab.at[step, :, :, :, lanes(mine)], own_sem.at[step])

    def slab_arrival(step, dy, dc):
        py, pc = line_peer(dy, dc)
        index = py * 2 + pc
        return pltpu.make_async_remote_copy(
            src_ref=weight.at[:, :, pl.ds(0, WIDTH), :],
            dst_ref=slab.at[step, :, :, :, lanes(index)],
            send_sem=slab_out.at[step, dy * 2 + dc], recv_sem=slab_sem.at[step, index],
            device_id=device(x, py, z, pc), device_id_type=MESH)

    def share_copy(step, dx, dz):
        px, pz = plane_peer(dx, dz)
        return pltpu.make_async_remote_copy(
            src_ref=sent.at[step, px * 4 + pz], dst_ref=got.at[step, spot],
            send_sem=got_out.at[step, dx * 4 + dz], recv_sem=got_sem.at[step, spot],
            device_id=device(px, y, pz, core), device_id_type=MESH)

    def share_arrival(step, dx, dz):
        px, pz = plane_peer(dx, dz)
        index = px * 4 + pz
        return pltpu.make_async_remote_copy(
            src_ref=sent.at[step, index], dst_ref=got.at[step, index],
            send_sem=got_out.at[step, dx * 4 + dz], recv_sem=got_sem.at[step, index],
            device_id=device(px, y, pz, core), device_id_type=MESH)

    def send_slab(step):
        slab_own(step).start()
        for dy, dc in line:
            slab_copy(step, dy, dc).start()

    own_feat = pltpu.make_async_copy(act, feat_slot(mine), out_sem.at[STEPS])
    own_feat.start()
    for order, (dy, dc) in enumerate(((2, 0), (1, 0), (3, 0), (0, 1))):
        py, pc = line_peer(dy, dc)
        feat_copy(act, mine, py, pc, order).start()
    for step in range(AHEAD):
        send_slab(step)
    for order, dy in enumerate((1, 3, 2)):
        py = lax.rem(y + dy, 4)
        index = py * 2 + core
        feat_copy(act, index, py, core, order).wait_recv()
        feat_copy(feat_slot(index), index, y, 1 - core, 4 + order).start()
    own_feat.wait()
    for dy in range(4):
        py = lax.rem(y + dy, 4)
        feat_copy(act, py * 2 + 1 - core, y, 1 - core, 3).wait_recv()

    anchors = [(points[g] + 1).astype(jnp.float32) * 0.125 for g in range(8)]

    def out_copy(step):
        rows = pl.ds(pl.multiple_of(step * WIDTH, WIDTH), WIDTH)
        return pltpu.make_async_copy(total.at[rows], out.at[0, rows], out_sem.at[step])

    def finish(step):
        for dx, dz in plane:
            share_arrival(step, dx, dz).wait_recv()

        def add(tile, carry):
            rows = pl.ds(pl.multiple_of(tile * 16, 16), 16)
            value = sent[step, spot, rows, :].astype(jnp.float32)
            for dx, dz in plane:
                px, pz = plane_peer(dx, dz)
                value = value + got[step, px * 4 + pz, rows, :].astype(jnp.float32)
            total[pl.ds(pl.multiple_of(step * WIDTH + tile * 16, 16), 16), :] = value
            return carry

        lax.fori_loop(0, WIDTH // 16, add, 0)
        out_copy(step).start()

    def body(step, carry):
        @pl.when(step + AHEAD < STEPS)
        def _():
            send_slab(step + AHEAD)

        slab_own(step).wait()
        for dy, dc in line:
            slab_arrival(step, dy, dc).wait_recv()
        left = slab[step].reshape(8 * WIDTH, 1024)
        for k in range(2):
            prods[k] = jnp.dot(left, feats[k], preferred_element_type=jnp.float32).reshape(4, 2, WIDTH, 512)

        def combine(tile, carry):
            half = tile // (WIDTH // 16)
            rows = pl.ds(pl.multiple_of((tile % (WIDTH // 16)) * 16, 16), 16)
            for part in range(2):
                cols = pl.ds(part * 256, 256)
                terms = [prods[p // 4, p % 4, half, rows, cols] for p in range(8)]
                for g in range(8):
                    value = terms[7]
                    for p in range(6, -1, -1):
                        value = value * anchors[g] + terms[p]
                    sent[step, (g // 2) * 4 + half * 2 + g % 2, rows, cols] = value.astype(jnp.bfloat16)
            return carry

        lax.fori_loop(0, 2 * WIDTH // 16, combine, 0)
        for dx, dz in plane:
            share_copy(step, dx, dz).start()

        @pl.when(step >= LAG)
        def _():
            finish(step - LAG)

        return carry

    lax.fori_loop(0, STEPS, body, 0)
    lax.fori_loop(STEPS - LAG, STEPS, lambda step, c: (finish(step), c)[1], 0)

    for order, (dy, dc) in enumerate(((2, 0), (1, 0), (3, 0), (0, 1))):
        py, pc = line_peer(dy, dc)
        feat_copy(act, mine, py, pc, order).wait_send()
    for order, dy in enumerate((1, 3, 2)):
        index = lax.rem(y + dy, 4) * 2 + core
        feat_copy(feat_slot(index), index, y, 1 - core, 4 + order).wait_send()

    def drain(step, carry):
        for dy, dc in line:
            slab_copy(step, dy, dc).wait_send()
        for dx, dz in plane:
            share_copy(step, dx, dz).wait_send()
        out_copy(step).wait()
        return carry

    lax.fori_loop(0, STEPS, drain, 0)


def per_device(weight, activation, points):
    any_space = pl.BlockSpec(memory_space=pl.ANY)
    dma = pltpu.SemaphoreType.DMA
    return pl.pallas_call(
        kernel,
        out_shape=jax.ShapeDtypeStruct((1, ROWS, 512), jnp.float32),
        in_specs=[any_space, any_space, pl.BlockSpec(memory_space=pltpu.SMEM)],
        out_specs=any_space,
        scratch_shapes=[
            pltpu.VMEM((STEPS, 4, 2, WIDTH, 1024), jnp.bfloat16),
            pltpu.VMEM((2, 1024, 512), jnp.bfloat16),
            pltpu.VMEM((2, 4, 2, WIDTH, 512), jnp.float32),
            pltpu.VMEM((STEPS, 16, WIDTH, 512), jnp.bfloat16),
            pltpu.VMEM((STEPS, 16, WIDTH, 512), jnp.bfloat16),
            pltpu.VMEM((ROWS, 512), jnp.float32),
            dma((STEPS, 8)), dma((STEPS, 8)), dma((8,)), dma((7,)),
            dma((STEPS, 16)), dma((STEPS, 16)), dma((STEPS,)), dma((STEPS + 1,)),
        ],
        compiler_params=pltpu.CompilerParams(
            collective_id=0, has_side_effects=True, vmem_limit_bytes=48 * 2**20),
        name="coded_share",
    )(weight.reshape(4, 2, 4096, 128), activation, points)


def solution(mesh):
    placed = (P(None, None, ("grp", "mem")), P(None, ("grp", "mem"), None), P())
    return jax.shard_map(
        per_device, mesh=mesh, in_specs=placed, out_specs=P("grp", "mem", None), check_vma=False
    )
```

time: 306 us -> 135 us (0.44)
  Pallas kernels: 0 us -> 131 us
  waiting for transfers between devices: 119 us -> 0 us
  local copies, waits for them, and re-layouts: 64.4 us -> 2.58 us
  blocking collectives: 53.1 us -> 0 us
  matrix products: 26.3 us -> 0 us
  other arithmetic: 19.2 us -> 0 us
  between operations: 13.5 us -> 0.01 us
  starting transfers between devices: 9.46 us -> 0 us
    pallas_call x0 -> x1, Pallas kernels: none -> 131 us  [per_device(): pl.pallas_call(kernel, out_shape=jax.ShapeDtypeStruct((1, ROWS, 512), jnp...]
    all_to_all x1 -> x0, waiting for transfers between devices: 118 us -> none  [per_device(): lax.all_to_all(weight, 'mem', split_axis=1, concat_axis=2, tiled=True)]
    all_to_all x1 -> x0, blocking collectives: 53.1 us -> none  [sum_at_owner(): lax.all_to_all(pieces, axis, split_axis=0, concat_axis=0, tiled=True)]
    convert_element_type x8 -> x0, local copies, waits for them, and re-layouts: 43.2 us -> none  [the longest x6 32.4 us: code_stack(): raw_blocks[block].astype(jnp.float32)[None]]
    dot_general x1 -> x0, matrix products: 26.3 us -> none  [per_device(): jnp.einsum('grk,gkc->grc', coded_weight, coded_input, preferred_element_t...]
    unnamed x9 -> x5, local copies, waits for them, and re-layouts: 13.3 us -> 2.58 us
    convert_element_type x1 -> x0, other arithmetic: 9.95 us -> none  [code_stack(): total = factors[:, 0, None, None] * raw_blocks[0].astype(jnp.float32)[None]]
    all_to_all x1 -> x0, starting transfers between devices: 9.42 us -> none  [per_device(): lax.all_to_all(weight, 'mem', split_axis=1, concat_axis=2, tiled=True)]
  transfers between devices with their start and end apart: 2 -> 0, of which waited for: 1 -> 0; matrix products, arithmetic and copies ran while one was open for 20% -> 0% of each run, Pallas kernels for 0% -> 0%
where the time goes in v1:
time: 135 us; the launch traced here: 133 us
  Pallas kernels  131 us (97%)
  local copies, waits for them, and re-layouts  2.58 us (2%)
    pallas_call x1, Pallas kernels, per_device(): pl.pallas_call(kernel, out_shape=jax.ShapeDtypeStruct((1, ROWS, 512), jnp...  131 us

profile of v1, /device:TPU:1, one launch (start us, length us, event | category | flops | bytes accessed | tf_op | source)
XLA Modules:
  0.0 133.3 jit_solution(6480096866142563831)
XLA Ops:
  0.0 0.0 copy-start
  0.0 0.9 copy-done
  1.0 0.0 copy-start.1
  1.0 0.7 copy-done.1
  1.6 130.7 %coded_share.1 = f32[1,512,512]{2,1,0:T(8,128)S(1)} custom-call(bf16[4,2,4096,128]{3,2,1,0:T(8,128)(2,1)} %bitcast.1, bf16[2,128,512]{2,1,0:T(8,128)(2,1)S(1)} %copy-done, s32[8]{0:T(128)S(1)} %copy-done.1), custom_call_target="tpu_custom_call" | custom-call | tf_op jit(solution)/shard_map/coded_share/pallas_call | solution.py:202
  132.4 1.0 copy.5
Async XLA Ops:
  0.0 0.9 copy-start
  1.0 0.7 copy-start.1

commit v2 on v0

v2 whole, which is shorter than its diff:
```python
import jax
import jax.numpy as jnp
from jax import lax
from jax.experimental import pallas as pl
from jax.experimental.pallas import tpu as pltpu
from jax.sharding import PartitionSpec as P

MESH = pl.DeviceIdType.MESH
STEPS = 8
WA = 32
WB = 16
BASE_B = STEPS * WA
AHEAD = 2
OTHER_A = (2, 5)
OTHER_B = (1, 4, 6)
LAG1 = 3
LAG2 = 6


def place():
    grp, mem = lax.axis_index("grp"), lax.axis_index("mem")
    return grp // 2, (mem // 2) % 4, (mem // 8) * 2 + grp % 2, mem % 2


def device(x, y, z, core):
    return (x * 2 + z % 2, (z // 2) * 8 + y * 2 + core)


def kernel(weight, act, points, out, slab_a, slab_b, feats, prods, part, part_in, sums, sums_in, anchor_mem,
           slab_sem, slab_out, own_sem, feat_sem, feat_out, one_sem, two_sem, one_out, two_out, misc_sem):
    x, y, z, core = place()
    low = z % 2
    gather_order = [(d, e) for d in (2, 1, 3, 0) for e in (0, 1) if d or e]
    swap_order = [(d, e) for d in (2, 1, 3, 0) for e in (0, 1) if d or e]

    def at(xx, yy, zz, cc):
        return device(lax.rem(xx, 4), lax.rem(yy, 4), lax.rem(zz, 4), lax.rem(cc, 2))

    def swapped(e):
        return (z // 2) * 2 + lax.rem(low + e, 2)

    peers = [at(x, y + d, z, core + e) for d in range(4) for e in range(2) if d or e]
    peers += [at(x, y, z + d, core + e) for d in range(1, 4) for e in range(2)]
    peers += [at(x + d, y, z, core) for d in range(1, 4)]
    peers += [at(x, y + d, swapped(1), core) for d in range(1, 4)]
    peers += [at(x + d, y, swapped(1), core) for d in range(1, 4)]
    barrier = pltpu.get_barrier_semaphore()
    for peer in peers:
        pl.semaphore_signal(barrier, inc=1, device_id=peer, device_id_type=MESH)
    pl.semaphore_wait(barrier, len(peers))

    def lanes(index):
        return pl.ds(pl.multiple_of(index * 128, 128), 128)

    def line_at(kind, d, e):
        return at(x, y + d, z, core + e) if kind == 0 else at(x, y, z + d, core + e)

    def line_pos(kind):
        return y if kind == 0 else z

    def line_index(kind, d, e):
        return lax.rem(line_pos(kind) + d, 4) * 2 + lax.rem(core + e, 2)

    def feat_slot(kind, index):
        return feats.at[kind, :, lanes(index), :]

    def feat_copy(kind, source, index, d, e, order):
        return pltpu.make_async_remote_copy(
            src_ref=source, dst_ref=feat_slot(kind, index), send_sem=feat_out.at[kind, order],
            recv_sem=feat_sem.at[kind, index], device_id=line_at(kind, d, e), device_id_type=MESH)

    def rows_for(kind, step, d, e):
        pos, cc = lax.rem(line_pos(kind) + d, 4), lax.rem(core + e, 2)
        if kind == 0:
            start = pl.multiple_of(step * WA, WA)
            return weight.at[:, :, pos, cc, pl.ds(start, WA), :]
        start = pl.multiple_of(BASE_B + (pos % 2) * (STEPS * WB) + step * WB, WB)
        return weight.at[:, pos // 2, :, cc, pl.ds(start, WB), :]

    def slab_slot(kind, step, index):
        slab = slab_a if kind == 0 else slab_b
        return slab.at[step, :, :, :, lanes(index)]

    def slab_copy(kind, step, d, e):
        mine = line_index(kind, 0, 0)
        return pltpu.make_async_remote_copy(
            src_ref=rows_for(kind, step, d, e), dst_ref=slab_slot(kind, step, mine),
            send_sem=slab_out.at[kind, step, d * 2 + e], recv_sem=slab_sem.at[kind, step, mine],
            device_id=line_at(kind, d, e), device_id_type=MESH)

    def slab_arrival(kind, step, d, e):
        index = line_index(kind, d, e)
        return pltpu.make_async_remote_copy(
            src_ref=rows_for(kind, step, d, e), dst_ref=slab_slot(kind, step, index),
            send_sem=slab_out.at[kind, step, d * 2 + e], recv_sem=slab_sem.at[kind, step, index],
            device_id=line_at(kind, d, e), device_id_type=MESH)

    def slab_own(kind, step):
        return pltpu.make_async_copy(
            rows_for(kind, step, 0, 0), slab_slot(kind, step, line_index(kind, 0, 0)), own_sem.at[kind, step])

    def send_slab(kind, step):
        slab_own(kind, step).start()
        for d, e in gather_order:
            slab_copy(kind, step, d, e).start()

    def first_axis(kind, step):
        other = OTHER_A if kind == 0 else OTHER_B
        flag = jnp.int32(1)
        for k in other:
            flag = flag - (step == k).astype(jnp.int32)
        return flag

    def one_pos(kind, f):
        return f * x + (1 - f) * (z if kind == 0 else y)

    def one_at(kind, f, d):
        if kind == 0:
            return at(x + f * d, y, z + (1 - f) * d, core)
        return at(x + f * d, y + (1 - f) * d, z, core)

    def one_copy(kind, step, d):
        f = first_axis(kind, step)
        mine = one_pos(kind, f)
        return pltpu.make_async_remote_copy(
            src_ref=part.at[kind, step, lax.rem(mine + d, 4)], dst_ref=part_in.at[kind, step, mine],
            send_sem=one_out.at[kind, step, d], recv_sem=one_sem.at[kind, step, mine],
            device_id=one_at(kind, f, d), device_id_type=MESH)

    def one_arrival(kind, step, d):
        f = first_axis(kind, step)
        index = lax.rem(one_pos(kind, f) + d, 4)
        return pltpu.make_async_remote_copy(
            src_ref=part.at[kind, step, index], dst_ref=part_in.at[kind, step, index],
            send_sem=one_out.at[kind, step, d], recv_sem=one_sem.at[kind, step, index],
            device_id=one_at(kind, f, d), device_id_type=MESH)

    def two_pos(kind, f):
        return f * (z if kind == 0 else y) + (1 - f) * x

    def two_at(kind, f, d, e):
        if kind == 0:
            return at(x + (1 - f) * d, y, z + f * d, core)
        return at(x + (1 - f) * d, y + f * d, swapped(e), core)

    def two_rows(kind, f, d, e):
        pos = lax.rem(two_pos(kind, f) + d, 4)
        if kind == 0:
            return pl.ds(pl.multiple_of(pos * WA, WA), WA)
        zl = lax.rem(low + e, 2)
        sub = f * (zl * 4 + pos) + (1 - f) * (pos * 2 + zl)
        return pl.ds(pl.multiple_of(sub * WB, WB), WB)

    def two_slot(kind, f, d, e):
        pos = lax.rem(two_pos(kind, f) + d, 4)
        return pos if kind == 0 else pos * 2 + lax.rem(low + e, 2)

    def slot_rows(kind, slot):
        width = WA if kind == 0 else WB
        return pl.ds(pl.multiple_of(slot * width, width), width)

    def two_list(kind):
        return [(2, 0), (1, 0), (3, 0)] if kind == 0 else swap_order

    def two_copy(kind, step, d, e):
        f = first_axis(kind, step)
        mine = two_slot(kind, f, 0, 0)
        return pltpu.make_async_remote_copy(
            src_ref=sums.at[kind, step, two_rows(kind, f, d, e), :],
            dst_ref=sums_in.at[kind, step, slot_rows(kind, mine), :],
            send_sem=two_out.at[kind, step, d * 2 + e], recv_sem=two_sem.at[kind, step, mine],
            device_id=two_at(kind, f, d, e), device_id_type=MESH)

    def two_arrival(kind, step, d, e):
        f = first_axis(kind, step)
        slot = two_slot(kind, f, d, e)
        return pltpu.make_async_remote_copy(
            src_ref=sums.at[kind, step, two_rows(kind, f, d, e), :],
            dst_ref=sums_in.at[kind, step, slot_rows(kind, slot), :],
            send_sem=two_out.at[kind, step, d * 2 + e], recv_sem=two_sem.at[kind, step, slot],
            device_id=two_at(kind, f, d, e), device_id_type=MESH)

    points_copy = pltpu.make_async_copy(points, anchor_mem, misc_sem.at[0])
    points_copy.start()
    feat_order = [(2, 0), (1, 0), (3, 0), (0, 1)]
    own_feats = [pltpu.make_async_copy(act, feat_slot(kind, line_index(kind, 0, 0)), misc_sem.at[1 + kind]) for kind in range(2)]
    for order, (d, e) in enumerate(feat_order):
        for kind in range(2):
            feat_copy(kind, act, line_index(kind, 0, 0), d, e, order).start()
    for copy in own_feats:
        copy.start()
    for step in range(AHEAD):
        for kind in range(2):
            send_slab(kind, step)
    for order, d in enumerate((1, 3, 2)):
        for kind in range(2):
            index = line_index(kind, d, 0)
            feat_copy(kind, act, index, d, 0, order).wait_recv()
            feat_copy(kind, feat_slot(kind, index), index, 0, 1, 4 + order).start()
    points_copy.wait()
    for kind in range(2):
        own_feats[kind].wait()
        for d in range(4):
            feat_copy(kind, act, line_index(kind, d, 1), 0, 1, 3).wait_recv()

    anchors = [(anchor_mem[g] + 1).astype(jnp.float32) * 0.125 for g in range(8)]

    def produce(kind, step):
        f = first_axis(kind, step)
        slab_own(kind, step).wait()
        for d, e in gather_order:
            slab_arrival(kind, step, d, e).wait_recv()
        slab = slab_a if kind == 0 else slab_b
        left = slab[step].reshape(256, 1024)
        for k in range(2):
            prods[k] = jnp.dot(left, feats[kind, k], preferred_element_type=jnp.float32).reshape(4, 64, 512)

        def combine(tile, carry):
            rows = pl.ds(pl.multiple_of(tile * 16, 16), 16)
            for half in range(2):
                cols = pl.ds(half * 256, 256)
                terms = [prods[p // 4, p % 4, rows, cols] for p in range(8)]
                for g in range(8):
                    value = terms[7]
                    for p in range(6, -1, -1):
                        value = value * anchors[g] + terms[p]
                    gx, zl = g // 2, g % 2
                    if kind == 0:
                        zz, inner = (tile // 2) * 2 + zl, (tile % 2) * 16
                        owner = f * gx + (1 - f) * zz
                        row = (f * zz + (1 - f) * gx) * WA + inner
                    else:
                        owner = f * gx + (1 - f) * tile
                        row = (f * (zl * 4 + tile) + (1 - f) * (gx * 2 + zl)) * WB
                    part[kind, step, owner, pl.ds(pl.multiple_of(row, 16), 16), cols] = value.astype(jnp.bfloat16)
            return carry

        lax.fori_loop(0, 4, combine, 0)
        for d in (2, 1, 3):
            one_copy(kind, step, d).start()

    def middle(kind, step):
        f = first_axis(kind, step)
        for d in range(1, 4):
            one_arrival(kind, step, d).wait_recv()
        mine = one_pos(kind, f)

        def add(tile, carry):
            rows = pl.ds(pl.multiple_of(tile * 16, 16), 16)
            value = part[kind, step, mine, rows, :].astype(jnp.float32)
            for d in range(1, 4):
                value = value + part_in[kind, step, lax.rem(mine + d, 4), rows, :].astype(jnp.float32)
            sums[kind, step, rows, :] = value.astype(jnp.bfloat16)
            return carry

        lax.fori_loop(0, 8, add, 0)
        for d, e in two_list(kind):
            two_copy(kind, step, d, e).start()

    def last(kind, step):
        f = first_axis(kind, step)
        for d, e in two_list(kind):
            two_arrival(kind, step, d, e).wait_recv()
        own = sums[kind, step, two_rows(kind, f, 0, 0), :].astype(jnp.float32)
        if kind == 0:
            value = own
            for d in range(1, 4):
                value = value + sums_in[kind, step, slot_rows(kind, two_slot(kind, f, d, 0)), :].astype(jnp.float32)
            out[0, pl.ds(pl.multiple_of(step * WA, WA), WA), :] = value
        else:
            for e in range(2):
                value = own if e == 0 else None
                for d in range(4):
                    if d or e:
                        piece = sums_in[kind, step, slot_rows(kind, two_slot(kind, f, d, e)), :].astype(jnp.float32)
                        value = piece if value is None else value + piece
                row = BASE_B + lax.rem(low + e, 2) * (STEPS * WB) + step * WB
                out[0, pl.ds(pl.multiple_of(row, WB), WB), :] = value

    def body(step, carry):
        @pl.when(step + AHEAD < STEPS)
        def _():
            for kind in range(2):
                send_slab(kind, step + AHEAD)

        for kind in range(2):
            produce(kind, step)

            @pl.when(step >= LAG1)
            def _():
                middle(kind, step - LAG1)

        @pl.when(step >= LAG2)
        def _():
            for kind in range(2):
                last(kind, step - LAG2)

        return carry

    lax.fori_loop(0, STEPS, body, 0)
    def finish(step, carry):
        @pl.when(step < STEPS + LAG1)
        def _():
            for kind in range(2):
                middle(kind, step - LAG1)

        for kind in range(2):
            last(kind, step - LAG2)
        return carry

    lax.fori_loop(STEPS, STEPS + LAG2, finish, 0)

    for kind in range(2):
        for order, (d, e) in enumerate(feat_order):
            feat_copy(kind, act, line_index(kind, 0, 0), d, e, order).wait_send()
        for order, d in enumerate((1, 3, 2)):
            index = line_index(kind, d, 0)
            feat_copy(kind, feat_slot(kind, index), index, 0, 1, 4 + order).wait_send()

    def drain(step, carry):
        for kind in range(2):
            for d, e in gather_order:
                slab_copy(kind, step, d, e).wait_send()
            for d in range(1, 4):
                one_copy(kind, step, d).wait_send()
            for d, e in two_list(kind):
                two_copy(kind, step, d, e).wait_send()
        return carry

    lax.fori_loop(0, STEPS, drain, 0)


def per_device(weight, activation, points):
    hbm = pl.BlockSpec(memory_space=pltpu.HBM)
    dma = pltpu.SemaphoreType.DMA
    return pl.pallas_call(
        kernel,
        out_shape=jax.ShapeDtypeStruct((1, 512, 512), jnp.float32),
        in_specs=[hbm, hbm, hbm],
        out_specs=pl.BlockSpec(memory_space=pltpu.VMEM),
        scratch_shapes=[
            pltpu.VMEM((STEPS, 4, 2, WA, 1024), jnp.bfloat16),
            pltpu.VMEM((STEPS, 4, 4, WB, 1024), jnp.bfloat16),
            pltpu.VMEM((2, 2, 1024, 512), jnp.bfloat16),
            pltpu.VMEM((2, 4, 64, 512), jnp.float32),
            pltpu.VMEM((2, STEPS, 4, 128, 512), jnp.bfloat16),
            pltpu.VMEM((2, STEPS, 4, 128, 512), jnp.bfloat16),
            pltpu.VMEM((2, STEPS, 128, 512), jnp.bfloat16),
            pltpu.VMEM((2, STEPS, 128, 512), jnp.bfloat16),
            pltpu.SMEM((8,), jnp.int32),
            dma((2, STEPS, 8)), dma((2, STEPS, 8)), dma((2, STEPS)), dma((2, 8)), dma((2, 7)),
            dma((2, STEPS, 4)), dma((2, STEPS, 8)), dma((2, STEPS, 4)), dma((2, STEPS, 8)), dma((3,)),
        ],
        compiler_params=pltpu.CompilerParams(
            collective_id=0, has_side_effects=True, vmem_limit_bytes=52 * 2**20),
        name="coded_share",
    )(weight.reshape(4, 2, 4, 2, 512, 128), activation, points)


def solution(mesh):
    placed = (P(None, None, ("grp", "mem")), P(None, ("grp", "mem"), None), P())
    return jax.shard_map(
        per_device, mesh=mesh, in_specs=placed, out_specs=P("grp", "mem", None), check_vma=False
    )
```

time: 306 us -> 110 us (0.36)
  waiting for transfers between devices: 119 us -> 0 us
  Pallas kernels: 0 us -> 107 us
  local copies, waits for them, and re-layouts: 64.4 us -> 2.58 us
  blocking collectives: 53.1 us -> 0 us
  matrix products: 26.3 us -> 0 us
  other arithmetic: 19.2 us -> 0 us
  between operations: 13.5 us -> 0.01 us
  starting transfers between devices: 9.46 us -> 0 us
    all_to_all x1 -> x0, waiting for transfers between devices: 118 us -> none  [per_device(): lax.all_to_all(weight, 'mem', split_axis=1, concat_axis=2, tiled=True)]
    pallas_call x0 -> x1, Pallas kernels: none -> 107 us  [per_device(): pl.pallas_call(kernel, out_shape=jax.ShapeDtypeStruct((1, 512, 512), jnp....]
    all_to_all x1 -> x0, blocking collectives: 53.1 us -> none  [sum_at_owner(): lax.all_to_all(pieces, axis, split_axis=0, concat_axis=0, tiled=True)]
    convert_element_type x8 -> x0, local copies, waits for them, and re-layouts: 43.2 us -> none  [the longest x6 32.4 us: code_stack(): raw_blocks[block].astype(jnp.float32)[None]]
    dot_general x1 -> x0, matrix products: 26.3 us -> none  [per_device(): jnp.einsum('grk,gkc->grc', coded_weight, coded_input, preferred_element_t...]
    unnamed x9 -> x5, local copies, waits for them, and re-layouts: 13.3 us -> 2.58 us
    convert_element_type x1 -> x0, other arithmetic: 9.95 us -> none  [code_stack(): total = factors[:, 0, None, None] * raw_blocks[0].astype(jnp.float32)[None]]
    all_to_all x1 -> x0, starting transfers between devices: 9.42 us -> none  [per_device(): lax.all_to_all(weight, 'mem', split_axis=1, concat_axis=2, tiled=True)]
  transfers between devices with their start and end apart: 2 -> 0, of which waited for: 1 -> 0; matrix products, arithmetic and copies ran while one was open for 20% -> 0% of each run, Pallas kernels for 0% -> 0%
where the time goes in v2:
time: 110 us
  Pallas kernels  107 us (97%)
  local copies, waits for them, and re-layouts  2.58 us (2%)
    pallas_call x1, Pallas kernels, per_device(): pl.pallas_call(kernel, out_shape=jax.ShapeDtypeStruct((1, 512, 512), jnp....  107 us
    unnamed x5, local copies, waits for them, and re-layouts  2.58 us

profile of v2, /device:TPU:1, one launch (start us, length us, event | category | flops | bytes accessed | tf_op | source)
XLA Modules:
  0.0 109.7 jit_solution(6642530330957701205)
XLA Ops:
  0.0 0.0 copy-start
  0.0 0.9 copy-done
  1.0 0.0 copy-start.1
  1.0 0.7 copy-done.1
  1.6 107.1 %coded_share.1 = f32[1,512,512]{2,1,0:T(8,128)S(1)} custom-call(bf16[4,2,4,2,512,128]{5,4,3,2,1,0:T(8,128)(2,1)} %bitcast.1, bf16[2,128,512]{2,1,0:T(8,128)(2,1)S(1)} %copy-done, s32[8]{0:T(128)S(1)} %copy-done.1), custom_call_target="tpu_custom_call" | custom-call | tf_op jit(solution)/shard_map/coded_share/pallas_call | solution.py:336
  108.7 1.0 copy.5
Async XLA Ops:
  0.0 0.9 copy-start
  1.0 0.7 copy-start.1

commit v3 on v2

v3 whole, which is shorter than its diff:
```python
import jax
import jax.numpy as jnp
from jax import lax
from jax.experimental import pallas as pl
from jax.experimental.pallas import tpu as pltpu
from jax.sharding import PartitionSpec as P

MESH = pl.DeviceIdType.MESH
STEPS = 8
WA = 32
WB = 16
BASE_B = STEPS * WA
AHEAD = 8
OTHER_A = (5, 6)
OTHER_B = (5, 6)
LAG0 = 2
LAG1 = 4
LAG2 = 8


def place():
    grp, mem = lax.axis_index("grp"), lax.axis_index("mem")
    return grp // 2, (mem // 2) % 4, (mem // 8) * 2 + grp % 2, mem % 2


def device(x, y, z, core):
    return (x * 2 + z % 2, (z // 2) * 8 + y * 2 + core)


def kernel(weight, act, points, out, slab_a, slab_b, feats, prods, part, relay, part_in, sums, sums_in, swap, anchor_mem,
           slab_sem, slab_out, feat_sem, pair_sem, feat_out, one_sem, one_out, two_sem, two_out, swap_sem, swap_out,
           misc_sem):
    x, y, z, core = place()
    low = z % 2
    gather_order = [(d, e) for d in (2, 1, 3, 0) for e in (0, 1) if d or e]

    def at(xx, yy, zz, cc):
        return device(lax.rem(xx, 4), lax.rem(yy, 4), lax.rem(zz, 4), lax.rem(cc, 2))

    peers = [at(x, y + d, z, core + e) for d in range(4) for e in range(2) if d or e]
    peers += [at(x, y, z + d, core + e) for d in range(1, 4) for e in range(2)]
    peers += [at(x + d, y, z, core) for d in range(1, 4)]
    barrier = pltpu.get_barrier_semaphore()
    for peer in peers:
        pl.semaphore_signal(barrier, inc=1, device_id=peer, device_id_type=MESH)
    pl.semaphore_wait(barrier, len(peers))

    def wait_for(ref, sem):
        pltpu.make_async_copy(ref, ref, sem).wait()

    def lanes(index):
        return pl.ds(pl.multiple_of(index * 128, 128), 128)

    def line_at(kind, d, e):
        return at(x, y + d, z, core + e) if kind == 0 else at(x, y, z + d, core + e)

    def line_pos(kind):
        return y if kind == 0 else z

    def line_index(kind, d, e):
        return lax.rem(line_pos(kind) + d, 4) * 2 + lax.rem(core + e, 2)

    def feat_slot(kind, index):
        return feats.at[kind, :, lanes(index), :]

    def feat_send(kind, d):
        return pltpu.make_async_remote_copy(
            src_ref=act, dst_ref=feat_slot(kind, line_index(kind, 0, 0)), send_sem=feat_out.at[kind],
            recv_sem=feat_sem.at[kind, d - 1], device_id=line_at(kind, d, 0), device_id_type=MESH)

    def feat_pair(kind, d):
        index = line_index(kind, d, 0)
        return pltpu.make_async_remote_copy(
            src_ref=act if d == 0 else feat_slot(kind, index), dst_ref=feat_slot(kind, index),
            send_sem=feat_out.at[kind], recv_sem=pair_sem.at[kind], device_id=line_at(kind, 0, 1), device_id_type=MESH)

    def rows_for(kind, step, d, e):
        pos, cc = lax.rem(line_pos(kind) + d, 4), lax.rem(core + e, 2)
        if kind == 0:
            start = pl.multiple_of(step * WA, WA)
            return weight.at[:, :, pos, cc, pl.ds(start, WA), :]
        start = pl.multiple_of(BASE_B + (pos % 2) * (STEPS * WB) + step * WB, WB)
        return weight.at[:, pos // 2, :, cc, pl.ds(start, WB), :]

    def slab_slot(kind, step, index):
        slab = slab_a if kind == 0 else slab_b
        return slab.at[step, :, :, :, lanes(index)]

    def slab_copy(kind, step, d, e):
        mine = line_index(kind, 0, 0)
        return pltpu.make_async_remote_copy(
            src_ref=rows_for(kind, step, d, e), dst_ref=slab_slot(kind, step, mine),
            send_sem=slab_out.at[kind], recv_sem=slab_sem.at[kind, step],
            device_id=line_at(kind, d, e), device_id_type=MESH)

    def slab_own(kind, step):
        return pltpu.make_async_copy(
            rows_for(kind, step, 0, 0), slab_slot(kind, step, line_index(kind, 0, 0)), slab_sem.at[kind, step])

    def send_slab(kind, step):
        slab_own(kind, step).start()
        for d, e in gather_order:
            slab_copy(kind, step, d, e).start()

    def first_axis(kind, step):
        other = OTHER_A if kind == 0 else OTHER_B
        flag = jnp.int32(1)
        for k in other:
            flag = flag - (step == k).astype(jnp.int32)
        return flag

    def one_pos(kind, f):
        return f * x + (1 - f) * (z if kind == 0 else y)

    def one_at(kind, f, d):
        if kind == 0:
            return at(x + f * d, y, z + (1 - f) * d, core)
        return at(x + f * d, y + (1 - f) * d, z, core)

    def hop(kind, step, order):
        f = first_axis(kind, step)
        mine = one_pos(kind, f)
        piece, half, way = ((2, 0, 1), (2, 1, 3), (1, 1, 1), (3, 0, 3), (1, 0, 1), (3, 1, 3))[order]
        rows = pl.ds(half * 64, 64)
        side = 0 if way == 1 else 1
        group = 0 if order < 2 else 1
        target = relay.at[kind, step, half] if order < 2 else part_in.at[kind, step, side, rows, :]
        return pltpu.make_async_remote_copy(
            src_ref=part.at[kind, step, lax.rem(mine + piece, 4), rows, :], dst_ref=target,
            send_sem=one_out.at[group], recv_sem=one_sem.at[kind, step, group],
            device_id=one_at(kind, f, way), device_id_type=MESH)

    def two_pos(kind, f):
        return f * (z if kind == 0 else y) + (1 - f) * x

    def two_at(kind, f, d):
        if kind == 0:
            return at(x + (1 - f) * d, y, z + f * d, core)
        return at(x + (1 - f) * d, y + f * d, z, core)

    def quarter(pos):
        return pl.ds(pl.multiple_of(lax.rem(pos, 4) * 32, 32), 32)

    def two_copy(kind, step, d):
        f = first_axis(kind, step)
        mine = two_pos(kind, f)
        return pltpu.make_async_remote_copy(
            src_ref=sums.at[kind, step, quarter(mine + d), :], dst_ref=sums_in.at[kind, step, quarter(mine), :],
            send_sem=two_out.at[0], recv_sem=two_sem.at[kind, step],
            device_id=two_at(kind, f, d), device_id_type=MESH)

    def row_b(which, step):
        return pl.ds(pl.multiple_of(BASE_B + which * (STEPS * WB) + step * WB, WB), WB)

    def swap_copy(step, which):
        rows = row_b(which, step)
        return pltpu.make_async_remote_copy(
            src_ref=swap.at[step], dst_ref=out.at[0, rows, :], send_sem=swap_out.at[0], recv_sem=swap_sem.at[0],
            device_id=at(x, y, (z // 2) * 2 + 1 - low, core), device_id_type=MESH)

    points_copy = pltpu.make_async_copy(points, anchor_mem, misc_sem.at[0])
    points_copy.start()
    own_feats = [pltpu.make_async_copy(act, feat_slot(kind, line_index(kind, 0, 0)), misc_sem.at[1 + kind]) for kind in range(2)]
    for d in (2, 1, 3):
        for kind in range(2):
            feat_send(kind, d).start()
    for kind in range(2):
        own_feats[kind].start()
        feat_pair(kind, 0).start()
    for step in range(AHEAD):
        for kind in range(2):
            send_slab(kind, step)
    for d in (1, 3, 2):
        for kind in range(2):
            wait_for(feat_slot(kind, line_index(kind, d, 0)), feat_sem.at[kind, 3 - d])
            feat_pair(kind, d).start()
    points_copy.wait()
    for kind in range(2):
        own_feats[kind].wait()
        wait_for(feats.at[kind, :, pl.ds(0, 512), :], pair_sem.at[kind])

    anchors = [(anchor_mem[g] + 1).astype(jnp.float32) * 0.125 for g in range(8)]

    def produce(kind, step):
        f = first_axis(kind, step)
        slab = slab_a if kind == 0 else slab_b
        wait_for(slab.at[step], slab_sem.at[kind, step])
        left = slab[step].reshape(256, 1024)
        for k in range(2):
            prods[k] = jnp.dot(left, feats[kind, k], preferred_element_type=jnp.float32).reshape(4, 64, 512)

        def combine(tile, carry):
            rows = pl.ds(pl.multiple_of(tile * 16, 16), 16)
            for half in range(2):
                cols = pl.ds(half * 256, 256)
                terms = [prods[p // 4, p % 4, rows, cols] for p in range(8)]
                for g in range(8):
                    value = terms[7]
                    for p in range(6, -1, -1):
                        value = value * anchors[g] + terms[p]
                    gx, zl = g // 2, g % 2
                    if kind == 0:
                        zz, inner = (tile // 2) * 2 + zl, (tile % 2) * 16
                        owner = f * gx + (1 - f) * zz
                        row = (f * zz + (1 - f) * gx) * WA + inner
                    else:
                        owner = f * gx + (1 - f) * tile
                        row = (f * tile + (1 - f) * gx) * 32 + zl * WB
                    part[kind, step, owner, pl.ds(pl.multiple_of(row, 16), 16), cols] = value.astype(jnp.bfloat16)
            return carry

        lax.fori_loop(0, 4, combine, 0)
        for order in range(4):
            hop(kind, step, order).start()

    def forward(kind, step):
        f = first_axis(kind, step)
        mine = one_pos(kind, f)
        wait_for(relay.at[kind, step], one_sem.at[kind, step, 0])
        for half in range(2):
            piece = lax.rem(mine + (1 if half == 0 else 3), 4)

            def add(tile, carry):
                rows = pl.ds(pl.multiple_of(tile * 16, 16), 16)
                where = pl.ds(pl.multiple_of(half * 64 + tile * 16, 16), 16)
                value = part[kind, step, piece, where, :].astype(jnp.float32) + relay[kind, step, half, rows, :].astype(jnp.float32)
                part[kind, step, piece, where, :] = value.astype(jnp.bfloat16)
                return carry

            lax.fori_loop(0, 4, add, 0)
            hop(kind, step, 4 + half).start()

    def middle(kind, step):
        f = first_axis(kind, step)
        wait_for(part_in.at[kind, step], one_sem.at[kind, step, 1])
        mine = one_pos(kind, f)

        def add(tile, carry):
            rows = pl.ds(pl.multiple_of(tile * 16, 16), 16)
            value = part[kind, step, mine, rows, :].astype(jnp.float32)
            for side in range(2):
                value = value + part_in[kind, step, side, rows, :].astype(jnp.float32)
            sums[kind, step, rows, :] = value.astype(jnp.bfloat16)
            return carry

        lax.fori_loop(0, 8, add, 0)
        for d in (2, 1, 3):
            two_copy(kind, step, d).start()

    def last(kind, step):
        f = first_axis(kind, step)
        mine = two_pos(kind, f)
        wait_for(sums_in.at[kind, step, pl.ds(0, 96), :], two_sem.at[kind, step])
        if kind == 0:
            value = sums[kind, step, quarter(mine), :].astype(jnp.float32)
            for d in range(1, 4):
                value = value + sums_in[kind, step, quarter(mine + d), :].astype(jnp.float32)
            out[0, pl.ds(pl.multiple_of(step * WA, WA), WA), :] = value
        else:
            for e in range(2):
                zl = lax.rem(low + e, 2)

                def rows(pos):
                    return pl.ds(pl.multiple_of(lax.rem(pos, 4) * 32 + zl * WB, WB), WB)

                value = sums[kind, step, rows(mine), :].astype(jnp.float32)
                for d in range(1, 4):
                    value = value + sums_in[kind, step, rows(mine + d), :].astype(jnp.float32)
                if e == 0:
                    out[0, row_b(low, step), :] = value
                else:
                    swap[step] = value
            swap_copy(step, low).start()

    def body(step, carry):
        @pl.when(step + AHEAD < STEPS)
        def _():
            for kind in range(2):
                send_slab(kind, step + AHEAD)

        for kind in range(2):
            produce(kind, step)

            @pl.when(step >= LAG0)
            def _():
                forward(kind, step - LAG0)

            @pl.when(step >= LAG1)
            def _():
                middle(kind, step - LAG1)

        @pl.when(step >= LAG2)
        def _():
            for kind in range(2):
                last(kind, step - LAG2)

        return carry

    lax.fori_loop(0, STEPS, body, 0)
    def finish(step, carry):
        @pl.when(step < STEPS + LAG0)
        def _():
            for kind in range(2):
                forward(kind, step - LAG0)

        @pl.when(step < STEPS + LAG1)
        def _():
            for kind in range(2):
                middle(kind, step - LAG1)

        for kind in range(2):
            last(kind, step - LAG2)
        return carry

    lax.fori_loop(STEPS, STEPS + LAG2, finish, 0)

    for kind in range(2):
        slab = slab_a if kind == 0 else slab_b
        wait_for(feats.at[kind, :, pl.ds(0, 896), :], feat_out.at[kind])
        wait_for(slab.at[:, :, :, :, pl.ds(0, 896)], slab_out.at[kind])
    wait_for(relay, one_out.at[0])
    wait_for(part_in, one_out.at[1])
    wait_for(sums_in.at[:, :, pl.ds(0, 96), :], two_out.at[0])
    wait_for(swap, swap_out.at[0])
    wait_for(swap, swap_sem.at[0])


def per_device(weight, activation, points):
    hbm = pl.BlockSpec(memory_space=pltpu.HBM)
    dma = pltpu.SemaphoreType.DMA
    return pl.pallas_call(
        kernel,
        out_shape=jax.ShapeDtypeStruct((1, 512, 512), jnp.float32),
        in_specs=[hbm, hbm, hbm],
        out_specs=pl.BlockSpec(memory_space=pltpu.VMEM),
        scratch_shapes=[
            pltpu.VMEM((STEPS, 4, 2, WA, 1024), jnp.bfloat16),
            pltpu.VMEM((STEPS, 4, 4, WB, 1024), jnp.bfloat16),
            pltpu.VMEM((2, 2, 1024, 512), jnp.bfloat16),
            pltpu.VMEM((2, 4, 64, 512), jnp.float32),
            pltpu.VMEM((2, STEPS, 4, 128, 512), jnp.bfloat16),
            pltpu.VMEM((2, STEPS, 2, 64, 512), jnp.bfloat16),
            pltpu.VMEM((2, STEPS, 2, 128, 512), jnp.bfloat16),
            pltpu.VMEM((2, STEPS, 128, 512), jnp.bfloat16),
            pltpu.VMEM((2, STEPS, 128, 512), jnp.bfloat16),
            pltpu.VMEM((STEPS, WB, 512), jnp.float32),
            pltpu.SMEM((8,), jnp.int32),
            dma((2, STEPS)), dma((2,)), dma((2, 3)), dma((2,)), dma((2,)),
            dma((2, STEPS, 2)), dma((2,)), dma((2, STEPS)), dma((1,)), dma((1,)), dma((1,)), dma((3,)),
        ],
        compiler_params=pltpu.CompilerParams(
            collective_id=0, has_side_effects=True, vmem_limit_bytes=52 * 2**20),
        name="coded_share",
    )(weight.reshape(4, 2, 4, 2, 512, 128), activation, points)


def solution(mesh):
    placed = (P(None, None, ("grp", "mem")), P(None, ("grp", "mem"), None), P())
    return jax.shard_map(
        per_device, mesh=mesh, in_specs=placed, out_specs=P("grp", "mem", None), check_vma=False
    )
```

time: 110 us -> 93.6 us (0.85)
  Pallas kernels: 107 us -> 90.9 us
    pallas_call x1, Pallas kernels: 107 us -> 90.9 us  [per_device(): pl.pallas_call(kernel, out_shape=jax.ShapeDtypeStruct((1, 512, 512), jnp....]
where the time goes in v3:
time: 93.6 us; the launch traced here: 93.4 us
  Pallas kernels  90.9 us (97%)
  local copies, waits for them, and re-layouts  2.58 us (3%)
    pallas_call x1, Pallas kernels, per_device(): pl.pallas_call(kernel, out_shape=jax.ShapeDtypeStruct((1, 512, 512), jnp....  90.9 us
    unnamed x5, local copies, waits for them, and re-layouts  2.58 us

profile of v3, /device:TPU:1, one launch (start us, length us, event | category | flops | bytes accessed | tf_op | source)
XLA Modules:
  0.0 93.4 jit_solution(12544311718139221835)
XLA Ops:
  0.0 0.0 copy-start
  0.0 0.9 %copy-done = bf16[2,128,512]{2,1,0:T(8,128)(2,1)S(1)} copy-done((bf16[2,128,512]{2,1,0:T(8,128)(2,1)S(1)}, bf16[2,128,512]{2,1,0:T(8,128)(2,1)}, u32[]{:S(2)}) %copy-start) | copy-done | bytes 262168
  1.0 0.0 copy-start.1
  1.0 0.7 copy-done.1
  1.6 90.9 %coded_share.1 = f32[1,512,512]{2,1,0:T(8,128)S(1)} custom-call(bf16[4,2,4,2,512,128]{5,4,3,2,1,0:T(8,128)(2,1)} %bitcast.1, bf16[2,128,512]{2,1,0:T(8,128)(2,1)S(1)} %copy-done, s32[8]{0:T(128)S(1)} %copy-done.1), custom_call_target="tpu_custom_call" | custom-call | tf_op jit(solution)/shard_map/coded_share/pallas_call | solution.py:331
  92.5 1.0 %copy.5 = f32[1,512,512]{2,1,0:T(8,128)} copy(f32[1,512,512]{2,1,0:T(8,128)S(1)} %coded_share.1) | data formatting | bytes 2097152
Async XLA Ops:
  0.0 0.9 %copy-start = (bf16[2,128,512]{2,1,0:T(8,128)(2,1)S(1)}, bf16[2,128,512]{2,1,0:T(8,128)(2,1)}, u32[]{:S(2)}) copy-start(bf16[2,128,512]{2,1,0:T(8,128)(2,1)} %act.1) | copy-start | bytes 786436
  1.0 0.7 copy-start.1

commit v4 on v3

--- a/solution.py
+++ b/solution.py
@@ -12,9 +12,9 @@
 BASE_B = STEPS * WA
 AHEAD = 8
 OTHER_A = (5, 6)
-OTHER_B = (5, 6)
+OTHER_B = (5, 7)
 LAG0 = 2
-LAG1 = 4
+LAG1 = 5
 LAG2 = 8
 
 
@@ -68,6 +68,13 @@
             src_ref=act, dst_ref=feat_slot(kind, line_index(kind, 0, 0)), send_sem=feat_out.at[kind],
             recv_sem=feat_sem.at[kind, d - 1], device_id=line_at(kind, d, 0), device_id_type=MESH)
 
+    def feat_pass(kind, d):
+        index, half = line_index(kind, 4 - d, 0), d // 2
+        piece = feats.at[kind, half, lanes(index), :]
+        return pltpu.make_async_remote_copy(
+            src_ref=piece, dst_ref=piece, send_sem=feat_out.at[kind],
+            recv_sem=feat_sem.at[kind, 1], device_id=line_at(kind, d, 0), device_id_type=MESH)
+
     def feat_pair(kind, d):
         index = line_index(kind, d, 0)
         return pltpu.make_async_remote_copy(
@@ -161,19 +168,25 @@
     points_copy = pltpu.make_async_copy(points, anchor_mem, misc_sem.at[0])
     points_copy.start()
     own_feats = [pltpu.make_async_copy(act, feat_slot(kind, line_index(kind, 0, 0)), misc_sem.at[1 + kind]) for kind in range(2)]
-    for d in (2, 1, 3):
+    for d in (1, 3):
         for kind in range(2):
             feat_send(kind, d).start()
     for kind in range(2):
         own_feats[kind].start()
         feat_pair(kind, 0).start()
+    for d in (1, 3):
+        for kind in range(2):
+            wait_for(feat_slot(kind, line_index(kind, 4 - d, 0)), feat_sem.at[kind, d - 1])
+            feat_pass(kind, d).start()
+    for d in (1, 3):
+        for kind in range(2):
+            feat_pair(kind, d).start()
     for step in range(AHEAD):
         for kind in range(2):
             send_slab(kind, step)
-    for d in (1, 3, 2):
-        for kind in range(2):
-            wait_for(feat_slot(kind, line_index(kind, d, 0)), feat_sem.at[kind, 3 - d])
-            feat_pair(kind, d).start()
+    for kind in range(2):
+        wait_for(feat_slot(kind, line_index(kind, 2, 0)), feat_sem.at[kind, 1])
+        feat_pair(kind, 2).start()
     points_copy.wait()
     for kind in range(2):
         own_feats[kind].wait()
@@ -278,7 +291,7 @@
             for kind in range(2):
                 send_slab(kind, step + AHEAD)
 
-        for kind in range(2):
+        for kind in (1, 0):
             produce(kind, step)
 
             @pl.when(step >= LAG0)
@@ -300,15 +313,15 @@
     def finish(step, carry):
         @pl.when(step < STEPS + LAG0)
         def _():
-            for kind in range(2):
+            for kind in (1, 0):
                 forward(kind, step - LAG0)
 
         @pl.when(step < STEPS + LAG1)
         def _():
-            for kind in range(2):
+            for kind in (1, 0):
                 middle(kind, step - LAG1)
 
-        for kind in range(2):
+        for kind in (1, 0):
             last(kind, step - LAG2)
         return carry
 

time: 93.6 us -> 91.6 us (0.979)
  Pallas kernels: 90.9 us -> 88.9 us
    pallas_call x1, Pallas kernels: 90.9 us -> 88.9 us  [per_device(): pl.pallas_call(kernel, out_shape=jax.ShapeDtypeStruct((1, 512, 512), jnp....]
where the time goes in v4:
time: 91.6 us; the launch traced here: 91.5 us
  Pallas kernels  88.9 us (97%)
  local copies, waits for them, and re-layouts  2.58 us (3%)
    pallas_call x1, Pallas kernels, per_device(): pl.pallas_call(kernel, out_shape=jax.ShapeDtypeStruct((1, 512, 512), jnp....  88.9 us
    unnamed x5, local copies, waits for them, and re-layouts  2.58 us

profile of v4, /device:TPU:1, one launch (start us, length us, event | category | flops | bytes accessed | tf_op | source)
XLA Modules:
  0.0 91.5 jit_solution(5704887114296606999)
XLA Ops:
  0.0 0.0 copy-start
  0.0 0.9 %copy-done = bf16[2,128,512]{2,1,0:T(8,128)(2,1)S(1)} copy-done((bf16[2,128,512]{2,1,0:T(8,128)(2,1)S(1)}, bf16[2,128,512]{2,1,0:T(8,128)(2,1)}, u32[]{:S(2)}) %copy-start) | copy-done | bytes 262168
  1.0 0.0 copy-start.1
  1.0 0.7 copy-done.1
  1.6 88.9 %coded_share.1 = f32[1,512,512]{2,1,0:T(8,128)S(1)} custom-call(bf16[4,2,4,2,512,128]{5,4,3,2,1,0:T(8,128)(2,1)} %bitcast.1, bf16[2,128,512]{2,1,0:T(8,128)(2,1)S(1)} %copy-done, s32[8]{0:T(128)S(1)} %copy-done.1), custom_call_target="tpu_custom_call" | custom-call | tf_op jit(solution)/shard_map/coded_share/pallas_call | solution.py:344
  90.5 1.0 %copy.5 = f32[1,512,512]{2,1,0:T(8,128)} copy(f32[1,512,512]{2,1,0:T(8,128)S(1)} %coded_share.1) | data formatting | bytes 2097152
Async XLA Ops:
  0.0 0.9 %copy-start = (bf16[2,128,512]{2,1,0:T(8,128)(2,1)S(1)}, bf16[2,128,512]{2,1,0:T(8,128)(2,1)}, u32[]{:S(2)}) copy-start(bf16[2,128,512]{2,1,0:T(8,128)(2,1)} %act.1) | copy-start | bytes 786436
  1.0 0.7 copy-start.1

commit v5 on v4

--- a/solution.py
+++ b/solution.py
@@ -11,7 +11,7 @@
 WB = 16
 BASE_B = STEPS * WA
 AHEAD = 8
-OTHER_A = (5, 6)
+OTHER_A = (5, 6, 7)
 OTHER_B = (5, 7)
 LAG0 = 2
 LAG1 = 5
@@ -27,11 +27,12 @@
     return (x * 2 + z % 2, (z // 2) * 8 + y * 2 + core)
 
 
-def kernel(weight, act, points, out, slab_a, slab_b, feats, prods, part, relay, part_in, sums, sums_in, swap, anchor_mem,
+def kernel(weight, act, points, out, slab_a, slab_b, feats, prods, part, relay, part_in, sums, sums_in, swap, swap_in, anchor_mem,
            slab_sem, slab_out, feat_sem, pair_sem, feat_out, one_sem, one_out, two_sem, two_out, swap_sem, swap_out,
            misc_sem):
     x, y, z, core = place()
     low = z % 2
+    early = ((1, 0), (3, 0))
     gather_order = [(d, e) for d in (2, 1, 3, 0) for e in (0, 1) if d or e]
 
     def at(xx, yy, zz, cc):
@@ -159,10 +160,9 @@
     def row_b(which, step):
         return pl.ds(pl.multiple_of(BASE_B + which * (STEPS * WB) + step * WB, WB), WB)
 
-    def swap_copy(step, which):
-        rows = row_b(which, step)
-        return pltpu.make_async_remote_copy(
-            src_ref=swap.at[step], dst_ref=out.at[0, rows, :], send_sem=swap_out.at[0], recv_sem=swap_sem.at[0],
+    def swap_copy(step):
+        return pltpu.make_async_remote_copy(
+            src_ref=swap.at[step], dst_ref=swap_in.at[step], send_sem=swap_out.at[0], recv_sem=swap_sem.at[0],
             device_id=at(x, y, (z // 2) * 2 + 1 - low, core), device_id_type=MESH)
 
     points_copy = pltpu.make_async_copy(points, anchor_mem, misc_sem.at[0])
@@ -174,6 +174,9 @@
     for kind in range(2):
         own_feats[kind].start()
         feat_pair(kind, 0).start()
+    for d, e in early:
+        for kind in range(2):
+            slab_copy(kind, 0, d, e).start()
     for d in (1, 3):
         for kind in range(2):
             wait_for(feat_slot(kind, line_index(kind, 4 - d, 0)), feat_sem.at[kind, d - 1])
@@ -181,7 +184,12 @@
     for d in (1, 3):
         for kind in range(2):
             feat_pair(kind, d).start()
-    for step in range(AHEAD):
+    for kind in range(2):
+        slab_own(kind, 0).start()
+        for d, e in gather_order:
+            if (d, e) not in early:
+                slab_copy(kind, 0, d, e).start()
+    for step in range(1, AHEAD):
         for kind in range(2):
             send_slab(kind, step)
     for kind in range(2):
@@ -282,8 +290,8 @@
                 if e == 0:
                     out[0, row_b(low, step), :] = value
                 else:
-                    swap[step] = value
-            swap_copy(step, low).start()
+                    swap[step] = value.astype(jnp.bfloat16)
+            swap_copy(step).start()
 
     def body(step, carry):
         @pl.when(step + AHEAD < STEPS)
@@ -335,7 +343,9 @@
     wait_for(part_in, one_out.at[1])
     wait_for(sums_in.at[:, :, pl.ds(0, 96), :], two_out.at[0])
     wait_for(swap, swap_out.at[0])
-    wait_for(swap, swap_sem.at[0])
+    wait_for(swap_in, swap_sem.at[0])
+    half = pl.ds(pl.multiple_of(BASE_B + (1 - low) * (STEPS * WB), WB), STEPS * WB)
+    out[0, half, :] = swap_in[...].reshape(STEPS * WB, 512).astype(jnp.float32)
 
 
 def per_device(weight, activation, points):
@@ -356,7 +366,8 @@
             pltpu.VMEM((2, STEPS, 2, 128, 512), jnp.bfloat16),
             pltpu.VMEM((2, STEPS, 128, 512), jnp.bfloat16),
             pltpu.VMEM((2, STEPS, 128, 512), jnp.bfloat16),
-            pltpu.VMEM((STEPS, WB, 512), jnp.float32),
+            pltpu.VMEM((STEPS, WB, 512), jnp.bfloat16),
+            pltpu.VMEM((STEPS, WB, 512), jnp.bfloat16),
             pltpu.SMEM((8,), jnp.int32),
             dma((2, STEPS)), dma((2,)), dma((2, 3)), dma((2,)), dma((2,)),
             dma((2, STEPS, 2)), dma((2,)), dma((2, STEPS)), dma((1,)), dma((1,)), dma((1,)), dma((3,)),

time: 91.6 us -> 91.1 us (level)
  Pallas kernels: 88.9 us -> 87.6 us
    pallas_call x1, Pallas kernels: 88.9 us -> 87.6 us  [per_device(): pl.pallas_call(kernel, out_shape=jax.ShapeDtypeStruct((1, 512, 512), jnp....]
where the time goes in v5:
time: 91.1 us; the launch traced here: 90.2 us
  Pallas kernels  87.6 us (96%)
  local copies, waits for them, and re-layouts  2.58 us (3%)
    pallas_call x1, Pallas kernels, per_device(): pl.pallas_call(kernel, out_shape=jax.ShapeDtypeStruct((1, 512, 512), jnp....  87.6 us
    unnamed x5, local copies, waits for them, and re-layouts  2.58 us

profile of v5, /device:TPU:1, one launch (start us, length us, event | category | flops | bytes accessed | tf_op | source)
XLA Modules:
  0.0 90.2 jit_solution(7885796197341873041)
XLA Ops:
  0.0 0.0 copy-start
  0.0 0.9 %copy-done = bf16[2,128,512]{2,1,0:T(8,128)(2,1)S(1)} copy-done((bf16[2,128,512]{2,1,0:T(8,128)(2,1)S(1)}, bf16[2,128,512]{2,1,0:T(8,128)(2,1)}, u32[]{:S(2)}) %copy-start) | copy-done | bytes 262168
  1.0 0.0 copy-start.1
  1.0 0.7 copy-done.1
  1.6 87.6 %coded_share.1 = f32[1,512,512]{2,1,0:T(8,128)S(1)} custom-call(bf16[4,2,4,2,512,128]{5,4,3,2,1,0:T(8,128)(2,1)} %bitcast.1, bf16[2,128,512]{2,1,0:T(8,128)(2,1)S(1)} %copy-done, s32[8]{0:T(128)S(1)} %copy-done.1), custom_call_target="tpu_custom_call" | custom-call | tf_op jit(solution)/shard_map/coded_share/pallas_call | solution.py:354
  89.3 1.0 %copy.5 = f32[1,512,512]{2,1,0:T(8,128)} copy(f32[1,512,512]{2,1,0:T(8,128)S(1)} %coded_share.1) | data formatting | bytes 2097152
Async XLA Ops:
  0.0 0.9 %copy-start = (bf16[2,128,512]{2,1,0:T(8,128)(2,1)S(1)}, bf16[2,128,512]{2,1,0:T(8,128)(2,1)}, u32[]{:S(2)}) copy-start(bf16[2,128,512]{2,1,0:T(8,128)(2,1)} %act.1) | copy-start | bytes 786436
  1.0 0.7 copy-start.1

commit v6 on v5

--- a/solution.py
+++ b/solution.py
@@ -44,7 +44,6 @@
     barrier = pltpu.get_barrier_semaphore()
     for peer in peers:
         pl.semaphore_signal(barrier, inc=1, device_id=peer, device_id_type=MESH)
-    pl.semaphore_wait(barrier, len(peers))
 
     def wait_for(ref, sem):
         pltpu.make_async_copy(ref, ref, sem).wait()
@@ -168,11 +167,14 @@
     points_copy = pltpu.make_async_copy(points, anchor_mem, misc_sem.at[0])
     points_copy.start()
     own_feats = [pltpu.make_async_copy(act, feat_slot(kind, line_index(kind, 0, 0)), misc_sem.at[1 + kind]) for kind in range(2)]
+    for kind in range(2):
+        own_feats[kind].start()
+        slab_own(kind, 0).start()
+    pl.semaphore_wait(barrier, len(peers))
     for d in (1, 3):
         for kind in range(2):
             feat_send(kind, d).start()
     for kind in range(2):
-        own_feats[kind].start()
         feat_pair(kind, 0).start()
     for d, e in early:
         for kind in range(2):
@@ -185,7 +187,6 @@
         for kind in range(2):
             feat_pair(kind, d).start()
     for kind in range(2):
-        slab_own(kind, 0).start()
         for d, e in gather_order:
             if (d, e) not in early:
                 slab_copy(kind, 0, d, e).start()

time: 91.1 us -> 91.1 us (level)
  no operation moved by 1% of the time
where the time goes in v6:
time: 91.1 us; the launch traced here: 90.2 us
  Pallas kernels  87.6 us (96%)
  local copies, waits for them, and re-layouts  2.58 us (3%)
    pallas_call x1, Pallas kernels, per_device(): pl.pallas_call(kernel, out_shape=jax.ShapeDtypeStruct((1, 512, 512), jnp....  87.6 us
    unnamed x5, local copies, waits for them, and re-layouts  2.58 us

profile of v6, /device:TPU:1, one launch (start us, length us, event | category | flops | bytes accessed | tf_op | source)
XLA Modules:
  0.0 90.2 jit_solution(3665408657089485320)
XLA Ops:
  0.0 0.0 copy-start
  0.0 0.9 %copy-done = bf16[2,128,512]{2,1,0:T(8,128)(2,1)S(1)} copy-done((bf16[2,128,512]{2,1,0:T(8,128)(2,1)S(1)}, bf16[2,128,512]{2,1,0:T(8,128)(2,1)}, u32[]{:S(2)}) %copy-start) | copy-done | bytes 262168
  1.0 0.0 copy-start.1
  1.0 0.7 copy-done.1
  1.6 87.6 %coded_share.1 = f32[1,512,512]{2,1,0:T(8,128)S(1)} custom-call(bf16[4,2,4,2,512,128]{5,4,3,2,1,0:T(8,128)(2,1)} %bitcast.1, bf16[2,128,512]{2,1,0:T(8,128)(2,1)S(1)} %copy-done, s32[8]{0:T(128)S(1)} %copy-done.1), custom_call_target="tpu_custom_call" | custom-call | tf_op jit(solution)/shard_map/coded_share/pallas_call | solution.py:355
  89.3 1.0 %copy.5 = f32[1,512,512]{2,1,0:T(8,128)} copy(f32[1,512,512]{2,1,0:T(8,128)S(1)} %coded_share.1) | data formatting | bytes 2097152
Async XLA Ops:
  0.0 0.9 %copy-start = (bf16[2,128,512]{2,1,0:T(8,128)(2,1)S(1)}, bf16[2,128,512]{2,1,0:T(8,128)(2,1)}, u32[]{:S(2)}) copy-start(bf16[2,128,512]{2,1,0:T(8,128)(2,1)} %act.1) | copy-start | bytes 786436
  1.0 0.7 copy-start.1
